TPU v7x, 32 devices: a whole 2x2x4 slice. The times are simulated.
32 devices in a mesh: grp: 2 (over y), bn: 16 (over z, x, core).
Axes of the slice: x: 2, y: 2, z: 4, core: 2. Of those that a mesh axis runs over, the one named last changes fastest.
Arguments:
- images: bfloat16 [32, 19, 19, 384], P(('grp', 'bn')), parts along dimension 0, may hold values from -56 to 56
- expand_weight: bfloat16 [384, 2304], P('bn'), may hold values from -0.3125 to 0.3125
- expand_gain: float32 [2304], replicated, may hold values from 0.5 to 2
- expand_shift: float32 [2304], replicated, may hold values from -3 to 3
- depth_weight: bfloat16 [25, 2304], replicated, may hold values from -1.25 to 1.25
- depth_gain: float32 [2304], replicated, may hold values from 0.5 to 2
- depth_shift: float32 [2304], replicated, may hold values from -3 to 3
- squeeze_weight: bfloat16 [2304, 96], replicated, may hold values from -0.125 to 0.125
- squeeze_bias: float32 [96], replicated, may hold values from -4 to 4
- excite_weight: bfloat16 [96, 2304], replicated, may hold values from -0.625 to 0.625
- excite_bias: float32 [2304], replicated, may hold values from -4 to 4
- project_weight: bfloat16 [2304, 384], P('bn'), may hold values from -0.125 to 0.125
- project_gain: float32 [384], replicated, may hold values from 0.5 to 2
- project_shift: float32 [384], replicated, may hold values from -3 to 3
- group_table: int32 [32], P('grp'), parts along dimension 0, may hold values from 0 to 1, as said below
Outputs:
- block_output: bfloat16 [32, 19, 19, 384], P(('grp', 'bn')), parts along dimension 0
There are 2 independent parts, one for each index of `grp`. A program takes and returns all parts, laid end to end along the dimension named above; an argument that names none is the same for every part. Nothing has to cross between parts.
Inputs may be any that keep to these rules, and one draw needn't show every extreme that they name: `group_table`: each of the 2 statistics groups holds at least 4 images, placed anywhere among the images.
All inputs are finite; a program needn't handle non-finite values.
Results may differ from a plain program's by a relative error of at most 0.0065.
Values may be sent and summed in bfloat16 or wider, within the bound.
A program may use at most 64 MiB of HBM per device.

v0:
```python
import jax
import jax.numpy as jnp
from jax import lax
from jax.sharding import PartitionSpec as P

KERNEL = 5
STAT_GROUPS = 2
epsilon = 0.001


def normalize(values, centre, inverse, gain, shift):
    return (values.astype(jnp.float32) - centre) * inverse * gain + shift


def depthwise(widened, depth_weight, height, breadth):
    spatial = widened.reshape(height, breadth, widened.shape[-1])
    margin = KERNEL // 2
    padded = jnp.pad(spatial, ((margin, margin), (margin, margin), (0, 0)))
    accumulated = jnp.zeros(spatial.shape, jnp.float32)
    for row_shift in range(KERNEL):
        for col_shift in range(KERNEL):
            window = padded[row_shift : row_shift + height, col_shift : col_shift + breadth]
            accumulated = accumulated + window.astype(jnp.float32) * depth_weight[
                row_shift * KERNEL + col_shift
            ].astype(jnp.float32)
    return accumulated.reshape(height * breadth, spatial.shape[-1]).astype(jnp.bfloat16)


def group_moments(values, selector, population):
    totals = jnp.sum(values, axis=0, dtype=jnp.float32)
    squares = jnp.sum(jnp.square(values.astype(jnp.float32)), axis=0)
    weighted = selector[:, None, None] * jnp.stack([totals, squares])[None]
    summed = lax.psum(weighted, "bn")
    picked = jnp.sum(selector[:, None, None] * summed, axis=0)
    centre = picked[0] / population
    spread = picked[1] / population - centre * centre
    return (centre, lax.rsqrt(spread + epsilon))


def on_device(
    images,
    expand_weight,
    expand_gain,
    expand_shift,
    depth_weight,
    depth_gain,
    depth_shift,
    squeeze_weight,
    squeeze_bias,
    excite_weight,
    excite_bias,
    project_weight,
    project_gain,
    project_shift,
    group_table,
):
    height, breadth, channels = (images.shape[1], images.shape[2], images.shape[3])
    pixels = height * breadth
    flattened = images.reshape(pixels, channels)
    device_rank = lax.axis_index("bn")
    ranks_all = jnp.arange(group_table.shape[0], dtype=jnp.int32)
    my_group = jnp.sum(jnp.where(ranks_all == device_rank, group_table, 0))
    members = jnp.sum((group_table == my_group).astype(jnp.float32))
    population = members * pixels
    selector = (jnp.arange(STAT_GROUPS, dtype=jnp.int32) == my_group).astype(jnp.float32)
    inputs = flattened
    expanded = jnp.dot(
        inputs,
        lax.all_gather(expand_weight, "bn", axis=0, tiled=True),
        preferred_element_type=jnp.float32,
    ).astype(jnp.bfloat16)
    centre, inverse = group_moments(expanded, selector, population)
    widened = jax.nn.silu(normalize(expanded, centre, inverse, expand_gain, expand_shift)).astype(
        jnp.bfloat16
    )
    filtered = depthwise(widened, depth_weight, height, breadth)
    centre, inverse = group_moments(filtered, selector, population)
    activated = jax.nn.silu(normalize(filtered, centre, inverse, depth_gain, depth_shift)).astype(
        jnp.bfloat16
    )
    pooled = (jnp.sum(activated, axis=0, dtype=jnp.float32) / pixels).astype(jnp.bfloat16)[None, :]
    squeezed = jax.nn.silu(
        jnp.dot(pooled, squeeze_weight, preferred_element_type=jnp.float32) + squeeze_bias
    ).astype(jnp.bfloat16)
    excitation = jax.nn.sigmoid(
        jnp.dot(squeezed, excite_weight, preferred_element_type=jnp.float32) + excite_bias
    )
    gated_input = (activated * excitation).astype(jnp.bfloat16)
    inputs = gated_input
    projected = jnp.dot(
        inputs,
        lax.all_gather(project_weight, "bn", axis=0, tiled=True),
        preferred_element_type=jnp.float32,
    ).astype(jnp.bfloat16)
    centre, inverse = group_moments(projected, selector, population)
    output = flattened.astype(jnp.float32) + normalize(
        projected, centre, inverse, project_gain, project_shift
    )
    return output.astype(jnp.bfloat16).reshape(images.shape)


def solution(mesh):
    return jax.shard_map(
        on_device,
        mesh=mesh,
        in_specs=(
            P(("grp", "bn"), None, None, None),
            P("bn", None),
            P(),
            P(),
            P(),
            P(),
            P(),
            P(),
            P(),
            P(),
            P(),
            P("bn", None),
            P(),
            P(),
            P("grp"),
        ),
        out_specs=P(("grp", "bn"), None, None, None),
        check_vma=False,
    )
```

profile of v0, /device:TPU:0, one launch (start us, length us, event | category | flops | bytes accessed | tf_op | source)
XLA Modules:
  0.0 257.8 jit_solution(15007953222312947867)
XLA Ops:
  6.5 0.0 copy-start
  6.5 0.0 all-gather.3.cloned.1.call-start
  6.5 0.7 all-gather.3.cloned.1.call-update
  7.3 0.0 all-gather.5.cloned.1.call-start
  7.3 0.7 all-gather.5.cloned.1.call-update
  8.0 1.3 fusion.15
  9.3 0.6 compare_convert_fusion.1
  10.0 1.9 fusion.16
  11.9 1.9 convert_reduce_fusion.27
  13.7 1.1 convert_reduce_fusion.26
  14.9 1.1 reshape.239
  16.5 0.0 copy-start.2
  16.5 0.0 copy-start.3
  16.6 36.0 %all-gather.3.cloned.1.call-done = bf16[384,2304]{1,0:T(8,128)(2,1)} async-done(((bf16[24,2304]{1,0:T(8,128)(2,1)}), bf16[384,2304]{1,0:T(8,128)(2,1)}) %all-gather.3.cloned.1.call-update) | async-done | bytes 1769488 | tf_op jit(solution)/shard_map/all_gather | solution.py:69
  52.5 3.7 %convert_reduce_fusion = (f32[2304]{0:T(1024)S(1)}, f32[2304]{0:T(1024)S(1)}, bf16[361,2304]{1,0:T(8,128)(2,1)}) fusion(bf16[361,384]{1,0:T(8,128)(2,1)S(1)} %reshape.239, bf16[384,2304]{1,0:T(8,128)(2,1)} %all-gather.3.cloned.1.call-done), kind=kOutput, calls=%fused_computation.2 | convolution fusion | flops 642933504 | bytes 3728640 | tf_op jit(solution)/shard_map/dot_general | solution.py:67
  56.3 0.1 broadcast_multiply_fusion.1
  56.4 59.8 %psum.21 = f32[2,2,2304]{2,1,0:T(2,128)S(1)} all-reduce(f32[2,2,2304]{2,1,0:T(2,128)S(1)} %broadcast_multiply_fusion.1), channel_id=1, replica_groups=mesh['grp'=2,'bn'=16] {'bn'}, use_global_device_ids=true, to_apply=%region_3.4 | all-reduce | flops 9216 | bytes 73728 | tf_op jit(solution)/shard_map/psum | solution.py:33
  116.2 0.1 multiply_reduce_fusion.3
  116.3 0.1 fusion.26
  116.3 0.0 copy-done.2
  116.4 0.0 copy-done.3
  116.4 2.6 %fusion.9 = bf16[361,2304]{1,0:T(8,128)(2,1)S(1)} fusion(bf16[361,2304]{1,0:T(8,128)(2,1)} %get-tuple-element.43, f32[2304]{0:T(1024)S(1)} %copy-done.2, f32[2304]{0:T(1024)S(1)} %copy-done.3, f32[2304]{0:T(1024)S(1)} %get-tuple-element.39, f32[2304]{0:T(1024)S(1)} %get-tuple-element.38), kind=kLoop, calls=%fused_computation.17 | loop fusion | flops 8317440 | bytes 3363840 | tf_op jit(solution)/shard_map/convert_element_type | solution.py:73
  119.0 2.0 reshape.240
  121.0 32.3 %convert_reduce_fusion.2 = (f32[2304]{0:T(1024)S(1)}, f32[2304]{0:T(1024)S(1)}, bf16[19,19,2304]{2,1,0:T(8,128)(2,1)S(1)}) fusion(f32[2304]{0:T(1024)S(1)} %get-tuple-element.34, f32[2304]{0:T(1024)S(1)} %get-tuple-element.35, f32[2304]{0:T(1024)S(1)} %get-tuple-element.12, f32[2304]{0:T(1024)S(1)} %get-tuple-element.13, f32[2304]{0:T(1024)S(1)} %get-tuple-element.14, ...), kind=kLoop, calls=%fused_computation.20 | loop fusion | flops 65703168 | bytes 3575808 | tf_op jit(solution)/shard_map/reduce_sum | solution.py:30
  153.3 0.0 copy-start.4
  153.3 0.0 copy-start.5
  153.3 0.0 copy-start.1
  153.3 0.0 copy-start.9
  153.4 0.0 copy-start.6
  153.4 2.2 reshape.267
  155.6 0.1 broadcast_multiply_fusion
  155.7 57.9 %psum.22 = f32[2,2,2304]{2,1,0:T(2,128)S(1)} all-reduce(f32[2,2,2304]{2,1,0:T(2,128)S(1)} %broadcast_multiply_fusion), channel_id=1, replica_groups=mesh['grp'=2,'bn'=16] {'bn'}, use_global_device_ids=true, to_apply=%region_8.9 | all-reduce | flops 9216 | bytes 73728 | tf_op jit(solution)/shard_map/psum | solution.py:33
  213.6 0.1 multiply_reduce_fusion.2
  213.7 0.1 fusion.25
  213.7 0.0 copy-done.4
  213.7 0.0 copy-done.5
  213.8 1.6 convert_reduce_fusion.1
  215.3 0.0 copy-done
  215.3 0.0 copy-done.1
  215.4 0.0 copy-done.9
  215.4 0.4 convolution_reduce_fusion
  215.8 0.0 copy-done.6
  215.8 0.0 copy-start.7
  215.8 0.0 copy-start.8
  215.9 0.0 all-gather.5.cloned.1.call-done
  215.9 3.9 %fusion.24 = (f32[384]{0:T(512)S(1)}, f32[384]{0:T(512)S(1)}, f32[361,384]{1,0:T(8,128)S(1)}) fusion(bf16[2304,384]{1,0:T(8,128)(2,1)} %all-gather.5.cloned.1.call-done, f32[2304]{0:T(1024)S(1)} %add_divide_fusion, f32[2304]{0:T(1024)S(1)} %copy-done.4, f32[2304]{0:T(1024)S(1)} %copy-done.5, f32[2304]{0:T(1024)S(1)} %get-tuple-element.37, ...), kind=kOutput, calls=%fused_computation.106 | convolution fusion | flops 649452672 | bytes 5700096 | tf_op jit(solution)/shard_map/dot_general | solution.py:90
  219.8 0.1 broadcast_multiply_fusion.2
  219.9 30.0 %psum.23 = f32[2,2,384]{2,1,0:T(2,128)S(1)} all-reduce(f32[2,2,384]{2,1,0:T(2,128)S(1)} %broadcast_multiply_fusion.2), channel_id=1, replica_groups=mesh['grp'=2,'bn'=16] {'bn'}, use_global_device_ids=true, to_apply=%region_13.14 | all-reduce | flops 1536 | bytes 12288 | tf_op jit(solution)/shard_map/psum | solution.py:33
  249.9 0.1 multiply_reduce_fusion.4
  250.0 0.0 copy-done.7
  250.0 0.0 copy-done.8
  250.0 0.1 add_convert_fusion.1
  250.2 0.8 reshape.241
  (13 shorter events, 0.2 us)
Async XLA Ops:
  6.5 208.8 %copy-start = (bf16[96,2304]{1,0:T(8,128)(2,1)S(1)}, bf16[96,2304]{1,0:T(8,128)(2,1)}, u32[]{:S(2)}) copy-start(bf16[96,2304]{1,0:T(8,128)(2,1)} %param.24) | copy-start | bytes 1327108
  6.5 46.0 %all-gather.3.cloned.1.call-start = ((), (), s32[]{:S(2)}) async-start(), calls=%async_computation | async-start | bytes 1880064 | tf_op jit(solution)/shard_map/all_gather | solution.py:69
  7.3 208.6 %all-gather.5.cloned.1.call-start = ((), (), s32[]{:S(2)}) async-start(), calls=%async_computation.1 | async-start | bytes 1880064 | tf_op jit(solution)/shard_map/all_gather | solution.py:92
  16.5 99.8 %copy-start.2 = (f32[2304]{0:T(1024)S(1)}, f32[2304]{0:T(1024)}, u32[]{:S(2)}) copy-start(f32[2304]{0:T(1024)} %param.18) | copy-start | bytes 27652
  16.5 99.8 %copy-start.3 = (f32[2304]{0:T(1024)S(1)}, f32[2304]{0:T(1024)}, u32[]{:S(2)}) copy-start(f32[2304]{0:T(1024)} %param.17) | copy-start | bytes 27652
  153.3 60.4 %copy-start.4 = (f32[2304]{0:T(1024)S(1)}, f32[2304]{0:T(1024)}, u32[]{:S(2)}) copy-start(f32[2304]{0:T(1024)} %param.21) | copy-start | bytes 27652
  153.3 60.4 %copy-start.5 = (f32[2304]{0:T(1024)S(1)}, f32[2304]{0:T(1024)}, u32[]{:S(2)}) copy-start(f32[2304]{0:T(1024)} %param.20) | copy-start | bytes 27652
  153.3 62.0 %copy-start.1 = (bf16[2304,96]{0,1:T(8,128)(2,1)S(1)}, bf16[2304,96]{0,1:T(8,128)(2,1)}, u32[]{:S(2)}) copy-start(bf16[2304,96]{0,1:T(8,128)(2,1)} %param.22) | copy-start | bytes 1327108
  153.3 62.0 %copy-start.9 = (f32[96]{0:T(128)S(1)}, f32[96]{0:T(128)}, u32[]{:S(2)}) copy-start(f32[96]{0:T(128)} %param.23) | copy-start | bytes 1156
  153.4 62.5 %copy-start.6 = (f32[2304]{0:T(1024)S(1)}, f32[2304]{0:T(1024)}, u32[]{:S(2)}) copy-start(f32[2304]{0:T(1024)} %param.25) | copy-start | bytes 27652
  215.8 34.2 %copy-start.7 = (f32[384]{0:T(512)S(1)}, f32[384]{0:T(512)}, u32[]{:S(2)}) copy-start(f32[384]{0:T(512)} %param.28) | copy-start | bytes 4612
  215.8 34.2 %copy-start.8 = (f32[384]{0:T(512)S(1)}, f32[384]{0:T(512)}, u32[]{:S(2)}) copy-start(f32[384]{0:T(512)} %param.27) | copy-start | bytes 4612
Sparse Core Ops, SparseCore 0:
  9.5 42.9 all-gather.2
  54.7 39.2 all-gather.4
where the time goes:
time: 258 us
  blocking collectives  148 us (57%)
  other arithmetic  44.2 us (17%)
  waiting for transfers between devices  37.4 us (14%)
  between operations  14.3 us (6%)
  matrix products  8.06 us (3%)
  local copies, waits for them, and re-layouts  6.24 us (2%)
    psum x3, blocking collectives, group_moments(): summed = lax.psum(weighted, 'bn')  148 us
    all_gather x1, waiting for transfers between devices, on_device(): lax.all_gather(expand_weight, 'bn', axis=0, tiled=True)  36 us
    reduce_sum x1, other arithmetic, group_moments(): totals = jnp.sum(values, axis=0, dtype=jnp.float32)  32.3 us
  transfers between devices with their start and end apart: 2, of which 1 were waited for; matrix products, arithmetic and copies ran while one was open for 21% of the time, Pallas kernels for 0%

commit v1 on v0

--- a/solution.py
+++ b/solution.py
@@ -30,7 +30,7 @@
     totals = jnp.sum(values, axis=0, dtype=jnp.float32)
     squares = jnp.sum(jnp.square(values.astype(jnp.float32)), axis=0)
     weighted = selector[:, None, None] * jnp.stack([totals, squares])[None]
-    summed = lax.psum(weighted, "bn")
+    summed = jnp.sum(lax.all_gather(weighted, "bn"), axis=0)
     picked = jnp.sum(selector[:, None, None] * summed, axis=0)
     centre = picked[0] / population
     spread = picked[1] / population - centre * centre

time: 258 us -> 172 us (0.67)
  blocking collectives: 148 us -> 59.6 us
    psum x3 -> x0, blocking collectives: 148 us -> none  [group_moments(): summed = lax.psum(weighted, 'bn')]
    all_gather x0 -> x3, blocking collectives: none -> 59.6 us  [group_moments(): summed = jnp.sum(lax.all_gather(weighted, 'bn'), axis=0)]
  transfers between devices with their start and end apart: 2 -> 2, of which waited for: 1 -> 1; matrix products, arithmetic and copies ran while one was open for 21% -> 32% of each run, Pallas kernels for 0% -> 0%
where the time goes in v1:
time: 172 us; the launch traced here: 171 us
  blocking collectives  59.6 us (35%)
  other arithmetic  44.5 us (26%)
  waiting for transfers between devices  37.4 us (22%)
  between operations  14.3 us (8%)
  matrix products  9.07 us (5%)
  local copies, waits for them, and re-layouts  6.23 us (4%)
    all_gather x3, blocking collectives, group_moments(): summed = jnp.sum(lax.all_gather(weighted, 'bn'), axis=0)  59.6 us
    all_gather x1, waiting for transfers between devices, on_device(): lax.all_gather(expand_weight, 'bn', axis=0, tiled=True)  36 us
    reduce_sum x1, other arithmetic, group_moments(): totals = jnp.sum(values, axis=0, dtype=jnp.float32)  32.2 us
    dot_general x1, matrix products, on_device(): jnp.dot(inputs, lax.all_gather(project_weight, 'bn', axis=0, tiled=True),...  3.9 us
    dot_general x1, matrix products, on_device(): jnp.dot(inputs, lax.all_gather(expand_weight, 'bn', axis=0, tiled=True),...  3.73 us
  transfers between devices with their start and end apart: 2, of which 1 were waited for; matrix products, arithmetic and copies ran while one was open for 32% of the time, Pallas kernels for 0%

profile of v1, /device:TPU:0, one launch (start us, length us, event | category | flops | bytes accessed | tf_op | source)
XLA Modules:
  0.0 171.2 jit_solution(2425344217353091036)
XLA Ops:
  6.5 0.0 copy-start
  6.5 0.0 all-gather.3.cloned.1.call-start
  6.5 0.7 all-gather.3.cloned.1.call-update
  7.3 0.0 all-gather.5.cloned.1.call-start
  7.3 0.7 all-gather.5.cloned.1.call-update
  8.0 1.3 fusion.15
  9.3 0.6 compare_convert_fusion.1
  10.0 1.9 %fusion.16 = f32[]{:T(128)} fusion(s32[16]{0:T(128)} %param.29, s32[]{:T(128)} %fusion.15), kind=kLoop, calls=%fused_computation.98 | loop fusion | flops 47 | bytes 72 | tf_op jit(solution)/shard_map/reduce_sum | solution.py:63
  11.9 1.9 %convert_reduce_fusion.27 = (f32[2304]{0:T(1024)S(1)}, f32[2304]{0:T(1024)S(1)}, f32[2304]{0:T(1024)S(1)}, f32[2304]{0:T(1024)S(1)}, f32[2304]{0:T(1024)S(1)}, /...) fusion(bf16[25,2304]{1,0:T(8,128)(2,1)} %param.19), kind=kLoop, calls=%fused_computation.84 | loop fusion | flops 43776 | bytes 262656 | tf_op jit(solution)/shard_map/convert_element_type | solution.py:25
  13.7 1.1 convert_reduce_fusion.26
  14.9 1.1 reshape.248
  16.5 0.0 copy-start.1
  16.5 0.0 copy-start.2
  16.6 36.0 %all-gather.3.cloned.1.call-done = bf16[384,2304]{1,0:T(8,128)(2,1)} async-done(((bf16[24,2304]{1,0:T(8,128)(2,1)}), bf16[384,2304]{1,0:T(8,128)(2,1)}) %all-gather.3.cloned.1.call-update) | async-done | bytes 1769488 | tf_op jit(solution)/shard_map/all_gather | solution.py:69
  52.5 3.7 %convert_reduce_fusion = (f32[2304]{0:T(1024)S(1)}, f32[2304]{0:T(1024)S(1)}, bf16[361,2304]{1,0:T(8,128)(2,1)}) fusion(bf16[361,384]{1,0:T(8,128)(2,1)S(1)} %reshape.248, bf16[384,2304]{1,0:T(8,128)(2,1)} %all-gather.3.cloned.1.call-done), kind=kOutput, calls=%fused_computation.2 | convolution fusion | flops 642933504 | bytes 3728640 | tf_op jit(solution)/shard_map/dot_general | solution.py:67
  56.3 0.1 broadcast_multiply_fusion.1
  56.4 21.4 %all_gather.19 = f32[16,2,2,2304]{3,2,1,0:T(2,128)S(1)} all-gather(f32[1,2,2,2304]{3,2,1,0:T(2,128)S(1)} %broadcast_multiply_fusion.1), channel_id=1, replica_groups=mesh['grp'=2,'bn'=16] {'bn'}, dimensions={0}, use_global_device_ids=true | all-gather | bytes 626688 | tf_op jit(solution)/shard_map/all_gather | solution.py:33
  77.8 0.2 reduce_sum.138
  78.0 0.1 multiply_reduce_fusion.3
  78.0 0.1 fusion.26
  78.1 0.0 copy-done.1
  78.1 0.0 copy-done.2
  78.1 2.6 %fusion.9 = bf16[361,2304]{1,0:T(8,128)(2,1)S(1)} fusion(bf16[361,2304]{1,0:T(8,128)(2,1)} %get-tuple-element.43, f32[2304]{0:T(1024)S(1)} %copy-done.1, f32[2304]{0:T(1024)S(1)} %copy-done.2, f32[2304]{0:T(1024)S(1)} %get-tuple-element.39, f32[2304]{0:T(1024)S(1)} %get-tuple-element.38), kind=kLoop, calls=%fused_computation.17 | loop fusion | flops 8317440 | bytes 3363840 | tf_op jit(solution)/shard_map/convert_element_type | solution.py:73
  80.8 2.0 %reshape.249 = bf16[19,19,2304]{2,1,0:T(8,128)(2,1)} reshape(bf16[361,2304]{1,0:T(8,128)(2,1)S(1)} %fusion.9) | data formatting | bytes 3326976 | tf_op jit(solution)/shard_map/reshape | solution.py:16
  82.8 32.2 %convert_reduce_fusion.2 = (f32[2304]{0:T(1024)S(1)}, f32[2304]{0:T(1024)S(1)}, bf16[19,19,2304]{2,1,0:T(8,128)(2,1)S(1)}) fusion(f32[2304]{0:T(1024)S(1)} %get-tuple-element.34, f32[2304]{0:T(1024)S(1)} %get-tuple-element.35, f32[2304]{0:T(1024)S(1)} %get-tuple-element.12, f32[2304]{0:T(1024)S(1)} %get-tuple-element.13, f32[2304]{0:T(1024)S(1)} %get-tuple-element.14, ...), kind=kLoop, calls=%fused_computation.20 | loop fusion | flops 65703168 | bytes 3575808 | tf_op jit(solution)/shard_map/reduce_sum | solution.py:30
  115.0 0.0 copy-start.3
  115.0 0.0 copy-start.4
  115.0 0.0 copy-start.8
  115.0 2.2 %reshape.276 = f32[361,2304]{1,0:T(8,128)} reshape(bf16[19,19,2304]{2,1,0:T(8,128)(2,1)S(1)} %get-tuple-element.42) | data formatting | bytes 4990464 | tf_op jit(solution)/shard_map/convert_element_type | solution.py:12
  117.2 0.0 copy-start.5
  117.3 0.1 broadcast_multiply_fusion
  117.4 19.2 %all_gather.20 = f32[16,2,2,2304]{3,2,1,0:T(2,128)S(1)} all-gather(f32[1,2,2,2304]{3,2,1,0:T(2,128)S(1)} %broadcast_multiply_fusion), channel_id=1, replica_groups=mesh['grp'=2,'bn'=16] {'bn'}, dimensions={0}, use_global_device_ids=true | all-gather | bytes 626688 | tf_op jit(solution)/shard_map/all_gather | solution.py:33
  136.6 0.2 reduce_sum.143
  136.8 0.1 multiply_reduce_fusion.2
  136.9 0.1 fusion.25
  137.0 0.0 copy-done.3
  137.0 0.0 copy-done.4
  137.0 1.6 convert_reduce_fusion.1
  138.6 0.0 copy-done
  138.6 0.0 copy-done.8
  138.6 1.4 convolution_reduce_fusion
  140.0 0.0 copy-done.5
  140.1 0.0 copy-start.6
  140.1 0.0 copy-start.7
  140.1 0.0 all-gather.5.cloned.1.call-done
  140.1 3.9 %fusion.24 = (f32[384]{0:T(512)S(1)}, f32[384]{0:T(512)S(1)}, f32[361,384]{1,0:T(8,128)S(1)}) fusion(bf16[2304,384]{1,0:T(8,128)(2,1)} %all-gather.5.cloned.1.call-done, f32[2304]{0:T(1024)S(1)} %add_divide_fusion, f32[2304]{0:T(1024)S(1)} %copy-done.3, f32[2304]{0:T(1024)S(1)} %copy-done.4, f32[2304]{0:T(1024)S(1)} %get-tuple-element.37, ...), kind=kOutput, calls=%fused_computation.106 | convolution fusion | flops 649452672 | bytes 5700096 | tf_op jit(solution)/shard_map/dot_general | solution.py:90
  144.1 0.1 broadcast_multiply_fusion.2
  144.1 19.0 %all_gather.22 = f32[16,2,2,384]{3,2,1,0:T(2,128)S(1)} all-gather(f32[1,2,2,384]{3,2,1,0:T(2,128)S(1)} %broadcast_multiply_fusion.2), channel_id=1, replica_groups=mesh['grp'=2,'bn'=16] {'bn'}, dimensions={0}, use_global_device_ids=true | all-gather | bytes 104448 | tf_op jit(solution)/shard_map/all_gather | solution.py:33
  163.2 0.1 multiply_reduce_fusion.4
  163.3 0.0 copy-done.6
  163.3 0.0 copy-done.7
  163.3 0.1 add_convert_fusion.1
  163.5 0.8 reshape.250
  (14 shorter events, 0.2 us)
Async XLA Ops:
  6.5 132.0 %copy-start = (bf16[96,2304]{1,0:T(8,128)(2,1)S(1)}, bf16[96,2304]{1,0:T(8,128)(2,1)}, u32[]{:S(2)}) copy-start(bf16[96,2304]{1,0:T(8,128)(2,1)} %param.24) | copy-start | bytes 1327108
  6.5 46.0 %all-gather.3.cloned.1.call-start = ((), (), s32[]{:S(2)}) async-start(), calls=%async_computation | async-start | bytes 1880064 | tf_op jit(solution)/shard_map/all_gather | solution.py:69
  7.3 132.9 %all-gather.5.cloned.1.call-start = ((), (), s32[]{:S(2)}) async-start(), calls=%async_computation.1 | async-start | bytes 1880064 | tf_op jit(solution)/shard_map/all_gather | solution.py:92
  16.5 61.6 %copy-start.1 = (f32[2304]{0:T(1024)S(1)}, f32[2304]{0:T(1024)}, u32[]{:S(2)}) copy-start(f32[2304]{0:T(1024)} %param.18) | copy-start | bytes 27652
  16.5 61.6 %copy-start.2 = (f32[2304]{0:T(1024)S(1)}, f32[2304]{0:T(1024)}, u32[]{:S(2)}) copy-start(f32[2304]{0:T(1024)} %param.17) | copy-start | bytes 27652
  115.0 22.0 %copy-start.3 = (f32[2304]{0:T(1024)S(1)}, f32[2304]{0:T(1024)}, u32[]{:S(2)}) copy-start(f32[2304]{0:T(1024)} %param.21) | copy-start | bytes 27652
  115.0 22.0 %copy-start.4 = (f32[2304]{0:T(1024)S(1)}, f32[2304]{0:T(1024)}, u32[]{:S(2)}) copy-start(f32[2304]{0:T(1024)} %param.20) | copy-start | bytes 27652
  115.0 23.6 %copy-start.8 = (f32[96]{0:T(128)S(1)}, f32[96]{0:T(128)}, u32[]{:S(2)}) copy-start(f32[96]{0:T(128)} %param.23) | copy-start | bytes 1156
  117.2 22.8 %copy-start.5 = (f32[2304]{0:T(1024)S(1)}, f32[2304]{0:T(1024)}, u32[]{:S(2)}) copy-start(f32[2304]{0:T(1024)} %param.25) | copy-start | bytes 27652
  140.1 23.3 %copy-start.6 = (f32[384]{0:T(512)S(1)}, f32[384]{0:T(512)}, u32[]{:S(2)}) copy-start(f32[384]{0:T(512)} %param.28) | copy-start | bytes 4612
  140.1 23.3 %copy-start.7 = (f32[384]{0:T(512)S(1)}, f32[384]{0:T(512)}, u32[]{:S(2)}) copy-start(f32[384]{0:T(512)} %param.27) | copy-start | bytes 4612
Sparse Core Ops, SparseCore 0:
  9.5 42.9 all-gather.2
  54.7 39.7 all-gather.4
